TPU v7x, 1024 devices: a whole 4x4x32 slice. The times are simulated.
1024 devices in a mesh: gx: 16 (over y, z_hi), gy: 8 (over z_lo), gz: 8 (over x, core).
Axes of the slice: x: 4, y: 4, z: 32 (z_hi: 4, z_lo: 8; z = z_hi * 8 + z_lo), core: 2. Of those that a mesh axis runs over, the one named last changes fastest.
Arguments:
- populations: float32 [19, 128, 64, 1024], P(None, 'gx', 'gy', 'gz'), may hold values from 0.01 to 0.11
Outputs:
- populations_next: float32 [19, 128, 64, 1024], P(None, 'gx', 'gy', 'gz')
- moments_slab: float32 [4, 1024, 64, 128], P(None, ('gz', 'gx'), 'gy')
All inputs are finite; a program needn't handle non-finite values.
Results may differ from a plain program's by a relative error of at most 0.0003.
Values sent between devices are 32-bit elements; how exact they have to be, the bound alone decides.
No kernel may reach another device: no remote copies, remote signals or barrier semaphores. Data moves between devices by JAX's collectives and lax.ppermute only.
A program may use at most 32 MiB of HBM per device.

v0:
```python
from functools import reduce

import jax
import jax.numpy as jnp
from jax import lax
from jax.experimental import pallas as pl
from jax.experimental.pallas import tpu as pltpu
from jax.sharding import PartitionSpec as P


lattice_moves = [
    (0, 0, 0),
    (1, 0, 0),
    (-1, 0, 0),
    (0, 1, 0),
    (0, -1, 0),
    (0, 0, 1),
    (0, 0, -1),
    (1, 1, 0),
    (-1, -1, 0),
    (1, -1, 0),
    (-1, 1, 0),
    (1, 0, 1),
    (-1, 0, -1),
    (1, 0, -1),
    (-1, 0, 1),
    (0, 1, 1),
    (0, -1, -1),
    (0, 1, -1),
    (0, -1, 1),
]
lattice_weights = [1.0 / 3.0] + [1.0 / 18.0] * 6 + [1.0 / 36.0] * 12
relaxation = 1.6
TILE = (8, 128)
SHIFTS = (0, 1, 2, -1)
LONG = (
    ("far", {2: 2, 3: 2, 0: -1, 1: 1}),
    ("up", {0: 1, 1: 1, 2: 1, 3: 1}),
    ("down", {0: -1, 1: -1, 2: -1, 3: -1}),
    ("relay", {2: 1, 3: -1}),
)
PASSING = {"far": (2, 3)}
f32 = jnp.float32


def moving(axis, sign):
    return [i for i, move in enumerate(lattice_moves) if move[axis] == sign]


XP, XM = moving(0, 1), moving(0, -1)
YP, YM = moving(1, 1), moving(1, -1)
ZP, ZM = moving(2, 1), moving(2, -1)


def lanes():
    return lax.broadcasted_iota(jnp.int32, TILE, 1)


def rows():
    return lax.broadcasted_iota(jnp.int32, TILE, 0)


def roll_lanes(tile, shift):
    shift %= 128
    return pltpu.roll(tile, shift, axis=1) if shift else tile


def roll_rows(tile, shift):
    shift %= 8
    return pltpu.roll(tile, shift, axis=0) if shift else tile


def momenta(pieces):
    density = pieces[0]
    for piece in pieces[1:]:
        density = density + piece
    sums = []
    for axis in range(3):
        ups, downs = [pieces[i] for i in moving(axis, 1)], [pieces[i] for i in moving(axis, -1)]
        total = ups[0] - downs[0]
        for up, down in zip(ups[1:], downs[1:]):
            total = total + (up - down)
        sums.append(total)
    inverse = 1.0 / density
    return [density] + [total * inverse for total in sums]


def swap_lane_groups(tiles, width):
    tiles, step, lane = list(tiles), 1, lanes()
    while step < len(tiles):
        low = (lane // (width * step)) % 2 == 0
        for a in range(len(tiles)):
            if not a & step:
                b = a + step
                one, two = tiles[a], tiles[b]
                tiles[a] = jnp.where(low, one, roll_lanes(two, width * step))
                tiles[b] = jnp.where(low, roll_lanes(one, -width * step), two)
        step *= 2
    return tiles


def face_columns(pops_ref, faces, edge):
    tile = jnp.zeros(TILE, f32)
    for q, i in enumerate(faces):
        for x in range(8):
            column = q * 8 + x
            tile = jnp.where(lanes() == column, roll_lanes(pops_ref[i, x], column - edge), tile)
    return tile


def z_kernel(pops_ref, zp_ref, zm_ref):
    zp_ref[...] = face_columns(pops_ref, ZP, 127)
    zm_ref[...] = face_columns(pops_ref, ZM, 0)


def pre_kernel(pops_ref, load_ref, parcels):
    fields = [momenta([pops_ref[i, x] for i in range(19)]) for x in range(8)]
    planes = [swap_lane_groups([fields[x][m] for x in range(8)], 1) for m in range(4)]
    for half in range(2):
        sixteen = swap_lane_groups(planes[2 * half] + planes[2 * half + 1], 8)
        for part in range(16):
            parcels[part, half] = sixteen[part]
    zhi = lax.rem(lax.axis_index("gx"), 4)
    for y in range(4):
        for r, shift in enumerate(SHIFTS):
            if shift == 2:
                shift = jnp.where(zhi == 0, -2, 2)
            part = lax.rem(zhi + (4 * y + shift + 16), 16)
            for half in range(2):
                load_ref[y, r * 2 + half] = parcels[part, half]


def along_z(tile, i, x, columns):
    cz = lattice_moves[i][2]
    if not cz:
        return tile
    faces, column = columns[cz]
    at, edge = faces.index(i) * 8 + x, 127 if cz == 1 else 0
    return roll_lanes(jnp.where(lanes() == edge, roll_lanes(column, edge - at), tile), cz)


def along_y(tile, i, x, lines):
    cy = lattice_moves[i][1]
    if not cy:
        return tile
    faces, tiles = lines[cy]
    line = jnp.broadcast_to(tiles[faces.index(i)][x : x + 1, :], TILE)
    return roll_rows(jnp.where(rows() == (7 if cy == 1 else 0), line, tile), cy)


def y_kernel(pops_ref, zp_ref, zm_ref, first_ref, second_ref, work_ref):
    columns = {1: (ZP, zp_ref[...]), -1: (ZM, zm_ref[...])}
    for faces, out, y in ((YP, work_ref.at[1], 7), (YM, work_ref.at[0], 0)):
        for q, i in enumerate(faces):
            tile = jnp.zeros(TILE, f32)
            for x in range(8):
                line = along_z(pops_ref[i, x], i, x, columns)
                tile = jnp.where(rows() == x, roll_rows(line, x - y), tile)
            out[q] = tile
    odd = lax.rem(lax.axis_index("gy"), 2)
    first_ref[...] = work_ref[odd]
    second_ref[...] = work_ref[1 - odd]


def y_lines(first_ref, second_ref):
    odd = lax.rem(lax.axis_index("gy"), 2) == 1
    lines = {}
    for sign, faces in ((1, YP), (-1, YM)):
        one, two = (first_ref, second_ref) if sign == 1 else (second_ref, first_ref)
        lines[sign] = (faces, [jnp.where(odd, two[q], one[q]) for q in range(5)])
    return lines


def far_kernel(load_ref, far_ref):
    for y in range(4):
        for half in range(2):
            far_ref[2 * y + half] = load_ref[y, 4 + half]


def x_kernel(pops_ref, zp_ref, zm_ref, first_ref, second_ref, load_ref, up_ref, down_ref):
    columns = {1: (ZP, zp_ref[...]), -1: (ZM, zm_ref[...])}
    lines = y_lines(first_ref, second_ref)
    for y in range(4):
        for half in range(2):
            k = 2 * y + half
            up_ref[k] = load_ref[y, 2 + half]
            down_ref[k] = load_ref[y, 6 + half]
    for faces, out, x in ((XP, up_ref, 7), (XM, down_ref, 0)):
        for q, i in enumerate(faces):
            out[8 + q] = along_y(along_z(pops_ref[i, x], i, x, columns), i, x, lines)


def arrived(came, kinds, k):
    zhi = lax.rem(lax.axis_index("gx"), 4)
    tile = None
    for (kind, ways), ref in zip(LONG, came):
        if kind in kinds:
            ends = [(g + by) % 4 for g, by in ways.items()]
            ends = [end for end in ends if end not in PASSING.get(kind, ())]
            if not ends:
                continue
            if tile is None:
                tile = ref[k]
            else:
                tile = jnp.where(reduce(jnp.logical_or, [zhi == end for end in ends]), ref[k], tile)
    return tile


def collide_kernel(pops_ref, zp_ref, zm_ref, first_ref, second_ref, *refs):
    *came, out_ref = refs
    columns = {1: (ZP, zp_ref[...]), -1: (ZM, zm_ref[...])}
    lines = y_lines(first_ref, second_ref)
    for x in range(8):
        read = []
        for i, (cx, cy, cz) in enumerate(lattice_moves):
            source = x - cx
            if source < 0:
                tile = arrived(came, ("up",), 8 + XP.index(i))
            elif source > 7:
                tile = arrived(came, ("down",), 8 + XM.index(i))
            else:
                tile = along_y(along_z(pops_ref[i, source], i, source, columns), i, source, lines)
            read.append(tile)
        density, ux, uy, uz = momenta(read)
        common = 1.0 - 1.5 * (ux * ux + uy * uy + uz * uz)
        scaled = {w: (relaxation * w) * density for w in sorted(set(lattice_weights))}
        keep = 1.0 - relaxation
        out_ref[0, x] = keep * read[0] + scaled[lattice_weights[0]] * common
        for i in range(1, 19, 2):
            projected = None
            for c, u in zip(lattice_moves[i], (ux, uy, uz)):
                if c:
                    term = u if c == 1 else -u
                    projected = term if projected is None else projected + term
            weight = scaled[lattice_weights[i]]
            even = weight * (common + 4.5 * projected * projected)
            odd = weight * (3.0 * projected)
            out_ref[i, x] = keep * read[i] + (even + odd)
            out_ref[i + 1, x] = keep * read[i + 1] + (even - odd)


def post_kernel(load_ref, *refs):
    *came, out_ref, parcels = refs
    zhi = lax.rem(lax.axis_index("gx"), 4)
    for shift, kinds in zip(SHIFTS, ((), ("up",), ("far", "relay"), ("down",))):
        slot = lax.rem(zhi + (4 - shift), 4)
        for k in range(8):
            parcels[slot, k] = arrived(came, kinds, k) if shift else load_ref[k // 2, k % 2]
    for half in range(2):
        tiles = [parcels[part % 4, part // 4 * 2 + half] for part in range(16)]
        for k, tile in enumerate(swap_lane_groups(tiles, 8)):
            out_ref[2 * half + k // 8, k % 8] = tile


def call(kernel, out_shapes, args, scratch=()):
    vmem = pl.BlockSpec(memory_space=pltpu.VMEM)
    return pl.pallas_call(
        kernel,
        out_shape=[jax.ShapeDtypeStruct(s, f32) for s in out_shapes],
        in_specs=[vmem] * len(args),
        out_specs=[vmem] * len(out_shapes),
        scratch_shapes=list(scratch),
        compiler_params=pltpu.CompilerParams(vmem_limit_bytes=16 * 1024 * 1024),
    )(*args)


def shifted(x, axis, by):
    count = lax.axis_size(axis)
    return lax.ppermute(x, axis, [(i, (i + by) % count) for i in range(count)])


def hop(x, ways):
    pairs = [(g, (g + ways[g % 4]) % 16) for g in range(16) if g % 4 in ways]
    return lax.ppermute(x, "gx", pairs)


def swap(x, lower):
    pairs = [(i % 8, (i + 1) % 8) for i in range(lower, lower + 8, 2)]
    return lax.ppermute(x, "gy", pairs + [(j, i) for i, j in pairs])


def steps(populations):
    zp, zm = call(z_kernel, [TILE, TILE], (populations,))
    zp, zm = shifted(zp, "gz", 1), shifted(zm, "gz", -1)
    (load,) = call(pre_kernel, [(4, 8, 8, 128)], (populations,), [pltpu.VMEM((16, 2, 8, 128), f32)])
    groups = [[y * 4 + z for y in range(4)] for z in range(4)]
    load = lax.all_to_all(
        load.reshape(4, 8192), "gx", 0, 0, tiled=True, axis_index_groups=groups
    ).reshape(4, 8, 8, 128)
    first, second = call(
        y_kernel, [(5, 8, 128)] * 2, (populations, zp, zm), [pltpu.VMEM((2, 5, 8, 128), f32)]
    )
    first, second = swap(first, 7), swap(second, 0)
    (far,) = call(far_kernel, [(8, 8, 128)], (load,))
    up, down = call(
        x_kernel, [(13, 8, 128)] * 2, (populations, zp, zm, first, second, load)
    )
    message = {"up": up, "far": far, "down": down}
    came = []
    for kind, ways in LONG:
        came.append(hop(message[kind], ways))
        if kind == "far" and (0 in ways or 1 in ways):
            message["relay"] = came[-1]
    (populations_next,) = call(
        collide_kernel, [(19, 8, 8, 128)], (populations, zp, zm, first, second, *came)
    )
    (moments_slab,) = call(
        post_kernel, [(4, 8, 8, 128)], (load, *came), [pltpu.VMEM((4, 8, 8, 128), f32)]
    )
    return (populations_next, moments_slab)


def solution(mesh):
    return jax.shard_map(
        steps,
        mesh=mesh,
        in_specs=(P(None, "gx", "gy", "gz"),),
        out_specs=(P(None, "gx", "gy", "gz"), P(None, ("gz", "gx"), "gy", None)),
        check_vma=False,
    )
```

profile of v0, /device:TPU:19, one launch (start us, length us, event | category | flops | bytes accessed | tf_op | source)
XLA Modules:
  0.0 74.9 jit_solution(12828547609429345027)
XLA Ops:
  0.6 1.1 %copy-done = f32[19,8,8,128]{3,2,1,0:T(8,128)S(1)} copy-done((f32[19,8,8,128]{3,2,1,0:T(8,128)S(1)}, f32[19,8,8,128]{3,2,1,0:T(8,128)}, u32[]{:S(2)}) %copy-start) | copy-done | bytes 622616
  1.7 1.2 %shard_map.32 = f32[4,8,8,128]{3,2,1,0:T(8,128)} custom-call(f32[19,8,8,128]{3,2,1,0:T(8,128)S(1)} %copy-done), custom_call_target="tpu_custom_call" | custom-call | tf_op jit(solution)/shard_map/pallas_call | solution.py:257
  2.9 4.2 %all-to-all-start = ((f32[4,1,8192]{2,1,0:T(1,128)}), f32[4,1,8192]{2,1,0:T(1,128)S(1)}, u32[]{:S(2)}, u32[]{:S(2)}) async-start(f32[4,1,8192]{2,1,0:T(1,128)} %bitcast), calls=%async_computation | async-start | bytes 262144 | tf_op jit(solution)/shard_map/all_to_all | solution.py:287
  7.2 0.1 shard_map.30
  7.3 2.3 %collective-permute-start = (f32[8,128]{1,0:T(8,128)S(1)}, f32[8,128]{1,0:T(8,128)S(1)}, u32[]{:S(2)}, u32[]{:S(2)}) collective-permute-start(f32[8,128]{1,0:T(8,128)S(1)} %get-tuple-element.8), channel_id=1, source_target_pairs={{0,1},{1,2},{2,3},{3,4},{4,5},{5,6},{6,7},{7,0},{8,9},{9,10},{10,1... | collective-permute-start | bytes 12296 | tf_op jit(solution)/shard_map/ppermute | solution.py:269
  9.7 0.0 collective-permute-start.1
  9.7 0.8 %collective-permute-done.zp_ref = f32[8,128]{1,0:T(8,128)S(1)} collective-permute-done((f32[8,128]{1,0:T(8,128)S(1)}, f32[8,128]{1,0:T(8,128)S(1)}, u32[]{:S(2)}, u32[]{:S(2)}) %collective-permute-start) | collective-permute-done | bytes 4128 | tf_op jit(solution)/shard_map/ppermute | solution.py:269
  10.4 2.3 %collective-permute-done.1.zm_ref = f32[8,128]{1,0:T(8,128)S(1)} collective-permute-done((f32[8,128]{1,0:T(8,128)S(1)}, f32[8,128]{1,0:T(8,128)S(1)}, u32[]{:S(2)}, u32[]{:S(2)}) %collective-permute-start.1) | collective-permute-done | bytes 4128 | tf_op jit(solution)/shard_map/ppermute | solution.py:269
  12.7 0.2 shard_map.31
  12.9 12.9 %collective-permute-start.2 = (f32[5,8,128]{2,1,0:T(8,128)S(1)}, f32[5,8,128]{2,1,0:T(8,128)S(1)}, u32[]{:S(2)}, u32[]{:S(2)}) collective-permute-start(f32[5,8,128]{2,1,0:T(8,128)S(1)} %get-tuple-element.10), channel_id=1, source_target_pairs={{56,0},{8,16},{24,32},{40,48},{0,56},{16,8},{32,24},{48,40},{57,1}... | collective-permute-start | bytes 61448 | tf_op jit(solution)/shard_map/ppermute | solution.py:279
  25.8 1.9 %collective-permute-start.3 = (f32[5,8,128]{2,1,0:T(8,128)S(1)}, f32[5,8,128]{2,1,0:T(8,128)S(1)}, u32[]{:S(2)}, u32[]{:S(2)}) collective-permute-start(f32[5,8,128]{2,1,0:T(8,128)S(1)} %get-tuple-element.11), channel_id=1, source_target_pairs={{0,8},{16,24},{32,40},{48,56},{8,0},{24,16},{40,32},{56,48},{1,9},... | collective-permute-start | bytes 61448 | tf_op jit(solution)/shard_map/ppermute | solution.py:279
  27.7 0.0 all-to-all-done
  27.7 15.2 %collective-permute-start.4 = (f32[8,8,128]{2,1,0:T(8,128)S(1)}, f32[8,8,128]{2,1,0:T(8,128)S(1)}, u32[]{:S(2)}, u32[]{:S(2)}) collective-permute-start(f32[8,8,128]{2,1,0:T(8,128)S(1)} %shard_map.33), channel_id=1, source_target_pairs={{0,960},{64,128},{128,256},{192,320},{256,192},{320,384},{384,512}... | collective-permute-start | bytes 98312 | tf_op jit(solution)/shard_map/ppermute | solution.py:274
  42.9 0.0 collective-permute-done.2.first_ref
  43.0 0.0 collective-permute-done.3.second_ref
  43.0 0.1 shard_map.34
  43.1 8.2 %collective-permute-start.5 = (f32[13,8,128]{2,1,0:T(8,128)S(1)}, f32[13,8,128]{2,1,0:T(8,128)S(1)}, u32[]{:S(2)}, u32[]{:S(2)}) collective-permute-start(f32[13,8,128]{2,1,0:T(8,128)S(1)} %get-tuple-element.12), channel_id=1, source_target_pairs={{0,64},{64,128},{128,192},{192,256},{256,320},{320,384},{384,448},... | collective-permute-start | bytes 159752 | tf_op jit(solution)/shard_map/ppermute | solution.py:274
  51.3 6.7 %collective-permute-start.6 = (f32[13,8,128]{2,1,0:T(8,128)S(1)}, f32[13,8,128]{2,1,0:T(8,128)S(1)}, u32[]{:S(2)}, u32[]{:S(2)}) collective-permute-start(f32[13,8,128]{2,1,0:T(8,128)S(1)} %get-tuple-element.13), channel_id=1, source_target_pairs={{0,960},{64,0},{128,64},{192,128},{256,192},{320,256},{384,320},{4... | collective-permute-start | bytes 159752 | tf_op jit(solution)/shard_map/ppermute | solution.py:274
  58.0 0.0 collective-permute-done.4.refs_0_
  58.0 0.7 collective-permute-start.7
  58.7 0.0 collective-permute-done.5.refs_1_
  58.7 14.0 %collective-permute-done.6.refs_2_ = f32[13,8,128]{2,1,0:T(8,128)S(1)} collective-permute-done((f32[13,8,128]{2,1,0:T(8,128)S(1)}, f32[13,8,128]{2,1,0:T(8,128)S(1)}, u32[]{:S(2)}, u32[]{:S(2)}) %collective-permute-start.6) | collective-permute-done | bytes 53280 | tf_op jit(solution)/shard_map/ppermute | solution.py:274
  72.7 1.0 %shard_map.36 = f32[4,8,8,128]{3,2,1,0:T(8,128)} custom-call(f32[4,8,8,128]{3,2,1,0:T(8,128)S(1)} %bitcast.4, f32[8,8,128]{2,1,0:T(8,128)S(1)} %collective-permute-done.4.refs_0_, f32[13,8,128]{2,1,0:T(8,128)S(1)} %collective-permute-done.5.refs_1_, f32[13,8,128]{2,1,0:T(8,128)S(1)} %collective-permute-done.6.refs_2_, ...), custom_call_target="tpu_custom_call" | custom-call | tf_op jit(solution)/shard_map/pallas_call | solution.py:257
  73.7 1.2 %shard_map.35 = f32[19,8,8,128]{3,2,1,0:T(8,128)} custom-call(f32[19,8,8,128]{3,2,1,0:T(8,128)S(1)} %copy-done.1, f32[8,128]{1,0:T(8,128)S(1)} %collective-permute-done.zp_ref, f32[8,128]{1,0:T(8,128)S(1)} %collective-permute-done.1.zm_ref, f32[5,8,128]{2,1,0:T(8,128)S(1)} %collective-permute-done.2.first_ref, ...), custom_call_target="tpu_custom_call" | custom-call | tf_op jit(solution)/shard_map/pallas_call | solution.py:257
  (5 shorter events, 0.0 us)
Async XLA Ops:
  0.6 1.1 %copy-start = (f32[19,8,8,128]{3,2,1,0:T(8,128)S(1)}, f32[19,8,8,128]{3,2,1,0:T(8,128)}, u32[]{:S(2)}) copy-start(f32[19,8,8,128]{3,2,1,0:T(8,128)} %pops_ref.9) | copy-start | bytes 1867780
  1.7 5.5 %copy-start.1 = (f32[19,8,8,128]{3,2,1,0:T(8,128)S(1)}, f32[19,8,8,128]{3,2,1,0:T(8,128)}, u32[]{:S(2)}) copy-start(f32[19,8,8,128]{3,2,1,0:T(8,128)} %pops_ref.9) | copy-start | bytes 1867780
  2.9 24.8 %all-to-all-start = ((f32[4,1,8192]{2,1,0:T(1,128)}), f32[4,1,8192]{2,1,0:T(1,128)S(1)}, u32[]{:S(2)}, u32[]{:S(2)}) async-start(f32[4,1,8192]{2,1,0:T(1,128)} %bitcast), calls=%async_computation | async-start | bytes 262144 | tf_op jit(solution)/shard_map/all_to_all | solution.py:287
  7.3 3.1 %collective-permute-start = (f32[8,128]{1,0:T(8,128)S(1)}, f32[8,128]{1,0:T(8,128)S(1)}, u32[]{:S(2)}, u32[]{:S(2)}) collective-permute-start(f32[8,128]{1,0:T(8,128)S(1)} %get-tuple-element.8), channel_id=1, source_target_pairs={{0,1},{1,2},{2,3},{3,4},{4,5},{5,6},{6,7},{7,0},{8,9},{9,10},{10,1... | collective-permute-start | bytes 12296 | tf_op jit(solution)/shard_map/ppermute | solution.py:269
  9.7 3.0 %collective-permute-start.1 = (f32[8,128]{1,0:T(8,128)S(1)}, f32[8,128]{1,0:T(8,128)S(1)}, u32[]{:S(2)}, u32[]{:S(2)}) collective-permute-start(f32[8,128]{1,0:T(8,128)S(1)} %get-tuple-element.9), channel_id=1, source_target_pairs={{0,7},{1,0},{2,1},{3,2},{4,3},{5,4},{6,5},{7,6},{8,15},{9,8},{10,9... | collective-permute-start | bytes 12296 | tf_op jit(solution)/shard_map/ppermute | solution.py:269
  12.9 30.1 %collective-permute-start.2 = (f32[5,8,128]{2,1,0:T(8,128)S(1)}, f32[5,8,128]{2,1,0:T(8,128)S(1)}, u32[]{:S(2)}, u32[]{:S(2)}) collective-permute-start(f32[5,8,128]{2,1,0:T(8,128)S(1)} %get-tuple-element.10), channel_id=1, source_target_pairs={{56,0},{8,16},{24,32},{40,48},{0,56},{16,8},{32,24},{48,40},{57,1}... | collective-permute-start | bytes 61448 | tf_op jit(solution)/shard_map/ppermute | solution.py:279
  25.8 17.2 %collective-permute-start.3 = (f32[5,8,128]{2,1,0:T(8,128)S(1)}, f32[5,8,128]{2,1,0:T(8,128)S(1)}, u32[]{:S(2)}, u32[]{:S(2)}) collective-permute-start(f32[5,8,128]{2,1,0:T(8,128)S(1)} %get-tuple-element.11), channel_id=1, source_target_pairs={{0,8},{16,24},{32,40},{48,56},{8,0},{24,16},{40,32},{56,48},{1,9},... | collective-permute-start | bytes 61448 | tf_op jit(solution)/shard_map/ppermute | solution.py:279
  27.7 30.3 %collective-permute-start.4 = (f32[8,8,128]{2,1,0:T(8,128)S(1)}, f32[8,8,128]{2,1,0:T(8,128)S(1)}, u32[]{:S(2)}, u32[]{:S(2)}) collective-permute-start(f32[8,8,128]{2,1,0:T(8,128)S(1)} %shard_map.33), channel_id=1, source_target_pairs={{0,960},{64,128},{128,256},{192,320},{256,192},{320,384},{384,512}... | collective-permute-start | bytes 98312 | tf_op jit(solution)/shard_map/ppermute | solution.py:274
  43.1 15.6 %collective-permute-start.5 = (f32[13,8,128]{2,1,0:T(8,128)S(1)}, f32[13,8,128]{2,1,0:T(8,128)S(1)}, u32[]{:S(2)}, u32[]{:S(2)}) collective-permute-start(f32[13,8,128]{2,1,0:T(8,128)S(1)} %get-tuple-element.12), channel_id=1, source_target_pairs={{0,64},{64,128},{128,192},{192,256},{256,320},{320,384},{384,448},... | collective-permute-start | bytes 159752 | tf_op jit(solution)/shard_map/ppermute | solution.py:274
  51.3 21.4 %collective-permute-start.6 = (f32[13,8,128]{2,1,0:T(8,128)S(1)}, f32[13,8,128]{2,1,0:T(8,128)S(1)}, u32[]{:S(2)}, u32[]{:S(2)}) collective-permute-start(f32[13,8,128]{2,1,0:T(8,128)S(1)} %get-tuple-element.13), channel_id=1, source_target_pairs={{0,960},{64,0},{128,64},{192,128},{256,192},{320,256},{384,320},{4... | collective-permute-start | bytes 159752 | tf_op jit(solution)/shard_map/ppermute | solution.py:274
  58.0 14.7 %collective-permute-start.7 = (f32[8,8,128]{2,1,0:T(8,128)S(1)}, f32[8,8,128]{2,1,0:T(8,128)S(1)}, u32[]{:S(2)}, u32[]{:S(2)}) collective-permute-start(f32[8,8,128]{2,1,0:T(8,128)S(1)} %collective-permute-done.4.refs_0_), channel_id=1, source_target_pairs={{128,192},{192,128},{384,448},{448,384},{640,704},{704,640},{896,9... | collective-permute-start | bytes 98312 | tf_op jit(solution)/shard_map/ppermute | solution.py:274
where the time goes:
time: 75.3 us; the launch traced here: 74.9 us
  starting transfers between devices  52.1 us (69%)
  waiting for transfers between devices  17 us (23%)
  Pallas kernels  3.95 us (5%)
  local copies, waits for them, and re-layouts  1.07 us (1%)
    ppermute x4, starting transfers between devices, hop(): return lax.ppermute(x, 'gx', pairs)  30.8 us
    ppermute x2, starting transfers between devices, swap(): return lax.ppermute(x, 'gy', pairs + [(j, i) for i, j in pairs])  14.8 us
    ppermute x4, waiting for transfers between devices, hop(): return lax.ppermute(x, 'gx', pairs)  14 us
    all_to_all x1, starting transfers between devices, steps(): lax.all_to_all(load.reshape(4, 8192), 'gx', 0, 0, tiled=True, axis_index_...  4.24 us
    pallas_call x7, Pallas kernels, call(): pl.pallas_call(kernel, out_shape=[jax.ShapeDtypeStruct(s, f32) for s in o...  3.95 us
    ppermute x2, waiting for transfers between devices, shifted(): return lax.ppermute(x, axis, [(i, (i + by) % count) for i in range(count)])  3.03 us
    ppermute x2, starting transfers between devices, shifted(): return lax.ppermute(x, axis, [(i, (i + by) % count) for i in range(count)])  2.34 us
  transfers between devices with their start and end apart: 9, of which 3 were waited for; matrix products, arithmetic and copies ran while one was open for 0% of the time, Pallas kernels for 1%

commit v1 on v0

--- a/solution.py
+++ b/solution.py
@@ -33,13 +33,9 @@
 relaxation = 1.6
 TILE = (8, 128)
 SHIFTS = (0, 1, 2, -1)
-LONG = (
-    ("far", {2: 2, 3: 2, 0: -1, 1: 1}),
-    ("up", {0: 1, 1: 1, 2: 1, 3: 1}),
-    ("down", {0: -1, 1: -1, 2: -1, 3: -1}),
-    ("relay", {2: 1, 3: -1}),
-)
+LONG = (('far', {2: 2, 3: 2, 0: -1}, None), ('up', {0: 1, 1: 1, 2: 1, 3: 1}, None), ('down', {0: -1, 1: -1, 2: -1, 3: -1}, None), ('far', {1: 1}, None), ('relay', {3: -1}, 0), ('relay', {2: 1}, 3))
 PASSING = {"far": (2, 3)}
+FAR_DOWN = (0,)
 f32 = jnp.float32
 
 
@@ -124,7 +120,7 @@
     for y in range(4):
         for r, shift in enumerate(SHIFTS):
             if shift == 2:
-                shift = jnp.where(zhi == 0, -2, 2)
+                shift = jnp.where(reduce(jnp.logical_or, [zhi == g for g in FAR_DOWN]), -2, 2)
             part = lax.rem(zhi + (4 * y + shift + 16), 16)
             for half in range(2):
                 load_ref[y, r * 2 + half] = parcels[part, half]
@@ -193,7 +189,7 @@
 def arrived(came, kinds, k):
     zhi = lax.rem(lax.axis_index("gx"), 4)
     tile = None
-    for (kind, ways), ref in zip(LONG, came):
+    for (kind, ways, _), ref in zip(LONG, came):
         if kind in kinds:
             ends = [(g + by) % 4 for g, by in ways.items()]
             ends = [end for end in ends if end not in PASSING.get(kind, ())]
@@ -206,8 +202,7 @@
     return tile
 
 
-def collide_kernel(pops_ref, zp_ref, zm_ref, first_ref, second_ref, *refs):
-    *came, out_ref = refs
+def collide_kernel(pops_ref, zp_ref, zm_ref, first_ref, second_ref, came, out_ref):
     columns = {1: (ZP, zp_ref[...]), -1: (ZM, zm_ref[...])}
     lines = y_lines(first_ref, second_ref)
     for x in range(8):
@@ -239,8 +234,7 @@
             out_ref[i + 1, x] = keep * read[i + 1] + (even - odd)
 
 
-def post_kernel(load_ref, *refs):
-    *came, out_ref, parcels = refs
+def post_kernel(load_ref, came, out_ref, parcels):
     zhi = lax.rem(lax.axis_index("gx"), 4)
     for shift, kinds in zip(SHIFTS, ((), ("up",), ("far", "relay"), ("down",))):
         slot = lax.rem(zhi + (4 - shift), 4)
@@ -250,6 +244,12 @@
         tiles = [parcels[part % 4, part // 4 * 2 + half] for part in range(16)]
         for k, tile in enumerate(swap_lane_groups(tiles, 8)):
             out_ref[2 * half + k // 8, k % 8] = tile
+
+
+def last_kernel(pops_ref, zp_ref, zm_ref, first_ref, second_ref, load_ref, *refs):
+    *came, next_ref, slab_ref, parcels = refs
+    collide_kernel(pops_ref, zp_ref, zm_ref, first_ref, second_ref, came, next_ref)
+    post_kernel(load_ref, came, slab_ref, parcels)
 
 
 def call(kernel, out_shapes, args, scratch=()):
@@ -297,22 +297,24 @@
     )
     message = {"up": up, "far": far, "down": down}
     came = []
-    for kind, ways in LONG:
-        came.append(hop(message[kind], ways))
-        if kind == "far" and (0 in ways or 1 in ways):
-            message["relay"] = came[-1]
-    (populations_next,) = call(
-        collide_kernel, [(19, 8, 8, 128)], (populations, zp, zm, first, second, *came)
+    for kind, ways, first_step in LONG:
+        sent = message[kind] if first_step is None else came[first_step]
+        came.append(hop(sent, ways))
+    return call(
+        last_kernel,
+        [(19, 8, 8, 128), (4, 8, 8, 128)],
+        (populations, zp, zm, first, second, load, *came),
+        [pltpu.VMEM((4, 8, 8, 128), f32)],
     )
-    (moments_slab,) = call(
-        post_kernel, [(4, 8, 8, 128)], (load, *came), [pltpu.VMEM((4, 8, 8, 128), f32)]
-    )
-    return (populations_next, moments_slab)
+
+
+def on_device(populations):
+    return tuple(steps(populations))
 
 
 def solution(mesh):
     return jax.shard_map(
-        steps,
+        on_device,
         mesh=mesh,
         in_specs=(P(None, "gx", "gy", "gz"),),
         out_specs=(P(None, "gx", "gy", "gz"), P(None, ("gz", "gx"), "gy", None)),

time: 75.3 us -> 81 us (1.076)
  the two profiles are of different devices: /device:TPU:19 before, /device:TPU:704 now
where the time goes in v1:
time: 81 us; the launch traced here: 80.6 us
  starting transfers between devices  61.1 us (75%)
  waiting for transfers between devices  14.5 us (18%)
  Pallas kernels  3.14 us (4%)
  local copies, waits for them, and re-layouts  1.07 us (1%)
    ppermute x6, starting transfers between devices, hop(): return lax.ppermute(x, 'gx', pairs)  43.9 us
    ppermute x6, waiting for transfers between devices, hop(): return lax.ppermute(x, 'gx', pairs)  13.2 us
    ppermute x2, starting transfers between devices, swap(): return lax.ppermute(x, 'gy', pairs + [(j, i) for i, j in pairs])  9.72 us
    all_to_all x1, starting transfers between devices, steps(): lax.all_to_all(load.reshape(4, 8192), 'gx', 0, 0, tiled=True, axis_index_...  4.46 us
    pallas_call x6, Pallas kernels, call(): pl.pallas_call(kernel, out_shape=[jax.ShapeDtypeStruct(s, f32) for s in o...  3.14 us
    ppermute x2, starting transfers between devices, shifted(): return lax.ppermute(x, axis, [(i, (i + by) % count) for i in range(count)])  2.96 us
  transfers between devices with their start and end apart: 11, of which 3 were waited for; matrix products, arithmetic and copies ran while one was open for 0% of the time, Pallas kernels for 1%

profile of v1, /device:TPU:704, one launch (start us, length us, event | category | flops | bytes accessed | tf_op | source)
XLA Modules:
  0.0 80.6 jit_solution(7476226765522225162)
XLA Ops:
  0.6 1.1 %copy-done = f32[19,8,8,128]{3,2,1,0:T(8,128)S(1)} copy-done((f32[19,8,8,128]{3,2,1,0:T(8,128)S(1)}, f32[19,8,8,128]{3,2,1,0:T(8,128)}, u32[]{:S(2)}) %copy-start) | copy-done | bytes 622616
  1.7 1.2 %shard_map.32 = f32[4,8,8,128]{3,2,1,0:T(8,128)} custom-call(f32[19,8,8,128]{3,2,1,0:T(8,128)S(1)} %copy-done), custom_call_target="tpu_custom_call" | custom-call | tf_op jit(solution)/shard_map/pallas_call | solution.py:257
  2.9 4.5 %all-to-all-start = ((f32[4,1,8192]{2,1,0:T(1,128)}), f32[4,1,8192]{2,1,0:T(1,128)S(1)}, u32[]{:S(2)}, u32[]{:S(2)}) async-start(f32[4,1,8192]{2,1,0:T(1,128)} %bitcast), calls=%async_computation | async-start | bytes 262144 | tf_op jit(solution)/shard_map/all_to_all | solution.py:287
  7.4 0.1 shard_map.30
  7.6 0.0 collective-permute-start
  7.6 2.9 %collective-permute-start.1 = (f32[8,128]{1,0:T(8,128)S(1)}, f32[8,128]{1,0:T(8,128)S(1)}, u32[]{:S(2)}, u32[]{:S(2)}) collective-permute-start(f32[8,128]{1,0:T(8,128)S(1)} %get-tuple-element.9), channel_id=1, source_target_pairs={{0,7},{1,0},{2,1},{3,2},{4,3},{5,4},{6,5},{7,6},{8,15},{9,8},{10,9... | collective-permute-start | bytes 12296 | tf_op jit(solution)/shard_map/ppermute | solution.py:269
  10.5 1.3 %collective-permute-done.zp_ref = f32[8,128]{1,0:T(8,128)S(1)} collective-permute-done((f32[8,128]{1,0:T(8,128)S(1)}, f32[8,128]{1,0:T(8,128)S(1)}, u32[]{:S(2)}, u32[]{:S(2)}) %collective-permute-start) | collective-permute-done | bytes 4128 | tf_op jit(solution)/shard_map/ppermute | solution.py:269
  11.8 0.0 collective-permute-done.1.zm_ref
  11.9 0.2 shard_map.31
  12.0 2.9 %collective-permute-start.2 = (f32[5,8,128]{2,1,0:T(8,128)S(1)}, f32[5,8,128]{2,1,0:T(8,128)S(1)}, u32[]{:S(2)}, u32[]{:S(2)}) collective-permute-start(f32[5,8,128]{2,1,0:T(8,128)S(1)} %get-tuple-element.10), channel_id=1, source_target_pairs={{56,0},{8,16},{24,32},{40,48},{0,56},{16,8},{32,24},{48,40},{57,1}... | collective-permute-start | bytes 61448 | tf_op jit(solution)/shard_map/ppermute | solution.py:279
  15.0 6.8 %collective-permute-start.3 = (f32[5,8,128]{2,1,0:T(8,128)S(1)}, f32[5,8,128]{2,1,0:T(8,128)S(1)}, u32[]{:S(2)}, u32[]{:S(2)}) collective-permute-start(f32[5,8,128]{2,1,0:T(8,128)S(1)} %get-tuple-element.11), channel_id=1, source_target_pairs={{0,8},{16,24},{32,40},{48,56},{8,0},{24,16},{40,32},{56,48},{1,9},... | collective-permute-start | bytes 61448 | tf_op jit(solution)/shard_map/ppermute | solution.py:279
  21.8 0.0 all-to-all-done
  21.8 1.3 %collective-permute-start.7 = (f32[8,8,128]{2,1,0:T(8,128)S(1)}, f32[8,8,128]{2,1,0:T(8,128)S(1)}, u32[]{:S(2)}, u32[]{:S(2)}) collective-permute-start(f32[8,8,128]{2,1,0:T(8,128)S(1)} %shard_map.33), channel_id=1, source_target_pairs={{64,128},{320,384},{576,640},{832,896},{65,129},{321,385},{577,641... | collective-permute-start | bytes 98312 | tf_op jit(solution)/shard_map/ppermute | solution.py:274
  23.1 7.5 %collective-permute-start.4 = (f32[8,8,128]{2,1,0:T(8,128)S(1)}, f32[8,8,128]{2,1,0:T(8,128)S(1)}, u32[]{:S(2)}, u32[]{:S(2)}) collective-permute-start(f32[8,8,128]{2,1,0:T(8,128)S(1)} %shard_map.33), channel_id=1, source_target_pairs={{0,960},{128,256},{192,320},{256,192},{384,512},{448,576},{512,448... | collective-permute-start | bytes 98312 | tf_op jit(solution)/shard_map/ppermute | solution.py:274
  30.6 0.0 collective-permute-done.2.first_ref
  30.6 0.1 shard_map.34
  30.7 19.3 %collective-permute-start.5 = (f32[13,8,128]{2,1,0:T(8,128)S(1)}, f32[13,8,128]{2,1,0:T(8,128)S(1)}, u32[]{:S(2)}, u32[]{:S(2)}) collective-permute-start(f32[13,8,128]{2,1,0:T(8,128)S(1)} %get-tuple-element.12), channel_id=1, source_target_pairs={{0,64},{64,128},{128,192},{192,256},{256,320},{320,384},{384,448},... | collective-permute-start | bytes 159752 | tf_op jit(solution)/shard_map/ppermute | solution.py:274
  50.1 1.9 %collective-permute-start.6 = (f32[13,8,128]{2,1,0:T(8,128)S(1)}, f32[13,8,128]{2,1,0:T(8,128)S(1)}, u32[]{:S(2)}, u32[]{:S(2)}) collective-permute-start(f32[13,8,128]{2,1,0:T(8,128)S(1)} %get-tuple-element.13), channel_id=1, source_target_pairs={{0,960},{64,0},{128,64},{192,128},{256,192},{320,256},{384,320},{4... | collective-permute-start | bytes 159752 | tf_op jit(solution)/shard_map/ppermute | solution.py:274
  52.0 12.6 %collective-permute-start.9 = (f32[8,8,128]{2,1,0:T(8,128)S(1)}, f32[8,8,128]{2,1,0:T(8,128)S(1)}, u32[]{:S(2)}, u32[]{:S(2)}) collective-permute-start(f32[8,8,128]{2,1,0:T(8,128)S(1)} %collective-permute-done.7.refs_3_), channel_id=1, source_target_pairs={{128,192},{384,448},{640,704},{896,960},{129,193},{385,449},{641,7... | collective-permute-start | bytes 98312 | tf_op jit(solution)/shard_map/ppermute | solution.py:274
  64.6 0.0 collective-permute-done.4.refs_0_
  64.7 1.3 %collective-permute-start.8 = (f32[8,8,128]{2,1,0:T(8,128)S(1)}, f32[8,8,128]{2,1,0:T(8,128)S(1)}, u32[]{:S(2)}, u32[]{:S(2)}) collective-permute-start(f32[8,8,128]{2,1,0:T(8,128)S(1)} %collective-permute-done.4.refs_0_), channel_id=1, source_target_pairs={{192,128},{448,384},{704,640},{960,896},{193,129},{449,385},{705,6... | collective-permute-start | bytes 98312 | tf_op jit(solution)/shard_map/ppermute | solution.py:274
  66.0 0.5 collective-permute-done.9.refs_5_
  66.5 12.7 %collective-permute-done.8.refs_4_ = f32[8,8,128]{2,1,0:T(8,128)S(1)} collective-permute-done((f32[8,8,128]{2,1,0:T(8,128)S(1)}, f32[8,8,128]{2,1,0:T(8,128)S(1)}, u32[]{:S(2)}, u32[]{:S(2)}) %collective-permute-start.8) | collective-permute-done | bytes 32800 | tf_op jit(solution)/shard_map/ppermute | solution.py:274
  79.2 1.4 %shard_map.35 = (f32[19,8,8,128]{3,2,1,0:T(8,128)}, f32[4,8,8,128]{3,2,1,0:T(8,128)}) custom-call(f32[19,8,8,128]{3,2,1,0:T(8,128)S(1)} %copy-done.1, f32[8,128]{1,0:T(8,128)S(1)} %collective-permute-done.zp_ref, f32[8,128]{1,0:T(8,128)S(1)} %collective-permute-done.1.zm_ref, f32[5,8,128]{2,1,0:T(8,128)S(1)} %collective-permute-done.2.first_ref, ...), custom_call_target="tpu_custom_call" | custom-call | tf_op jit(solution)/shard_map/pallas_call | solution.py:257
  (8 shorter events, 0.0 us)
Async XLA Ops:
  0.6 1.1 %copy-start = (f32[19,8,8,128]{3,2,1,0:T(8,128)S(1)}, f32[19,8,8,128]{3,2,1,0:T(8,128)}, u32[]{:S(2)}) copy-start(f32[19,8,8,128]{3,2,1,0:T(8,128)} %pops_ref.9) | copy-start | bytes 1867780
  1.7 5.7 %copy-start.1 = (f32[19,8,8,128]{3,2,1,0:T(8,128)S(1)}, f32[19,8,8,128]{3,2,1,0:T(8,128)}, u32[]{:S(2)}) copy-start(f32[19,8,8,128]{3,2,1,0:T(8,128)} %pops_ref.9) | copy-start | bytes 1867780
  2.9 18.8 %all-to-all-start = ((f32[4,1,8192]{2,1,0:T(1,128)}), f32[4,1,8192]{2,1,0:T(1,128)S(1)}, u32[]{:S(2)}, u32[]{:S(2)}) async-start(f32[4,1,8192]{2,1,0:T(1,128)} %bitcast), calls=%async_computation | async-start | bytes 262144 | tf_op jit(solution)/shard_map/all_to_all | solution.py:287
  7.6 4.3 %collective-permute-start = (f32[8,128]{1,0:T(8,128)S(1)}, f32[8,128]{1,0:T(8,128)S(1)}, u32[]{:S(2)}, u32[]{:S(2)}) collective-permute-start(f32[8,128]{1,0:T(8,128)S(1)} %get-tuple-element.8), channel_id=1, source_target_pairs={{0,1},{1,2},{2,3},{3,4},{4,5},{5,6},{6,7},{7,0},{8,9},{9,10},{10,1... | collective-permute-start | bytes 12296 | tf_op jit(solution)/shard_map/ppermute | solution.py:269
  7.6 4.3 %collective-permute-start.1 = (f32[8,128]{1,0:T(8,128)S(1)}, f32[8,128]{1,0:T(8,128)S(1)}, u32[]{:S(2)}, u32[]{:S(2)}) collective-permute-start(f32[8,128]{1,0:T(8,128)S(1)} %get-tuple-element.9), channel_id=1, source_target_pairs={{0,7},{1,0},{2,1},{3,2},{4,3},{5,4},{6,5},{7,6},{8,15},{9,8},{10,9... | collective-permute-start | bytes 12296 | tf_op jit(solution)/shard_map/ppermute | solution.py:269
  12.0 18.5 %collective-permute-start.2 = (f32[5,8,128]{2,1,0:T(8,128)S(1)}, f32[5,8,128]{2,1,0:T(8,128)S(1)}, u32[]{:S(2)}, u32[]{:S(2)}) collective-permute-start(f32[5,8,128]{2,1,0:T(8,128)S(1)} %get-tuple-element.10), channel_id=1, source_target_pairs={{56,0},{8,16},{24,32},{40,48},{0,56},{16,8},{32,24},{48,40},{57,1}... | collective-permute-start | bytes 61448 | tf_op jit(solution)/shard_map/ppermute | solution.py:279
  15.0 15.6 %collective-permute-start.3 = (f32[5,8,128]{2,1,0:T(8,128)S(1)}, f32[5,8,128]{2,1,0:T(8,128)S(1)}, u32[]{:S(2)}, u32[]{:S(2)}) collective-permute-start(f32[5,8,128]{2,1,0:T(8,128)S(1)} %get-tuple-element.11), channel_id=1, source_target_pairs={{0,8},{16,24},{32,40},{48,56},{8,0},{24,16},{40,32},{56,48},{1,9},... | collective-permute-start | bytes 61448 | tf_op jit(solution)/shard_map/ppermute | solution.py:279
  21.8 30.2 %collective-permute-start.7 = (f32[8,8,128]{2,1,0:T(8,128)S(1)}, f32[8,8,128]{2,1,0:T(8,128)S(1)}, u32[]{:S(2)}, u32[]{:S(2)}) collective-permute-start(f32[8,8,128]{2,1,0:T(8,128)S(1)} %shard_map.33), channel_id=1, source_target_pairs={{64,128},{320,384},{576,640},{832,896},{65,129},{321,385},{577,641... | collective-permute-start | bytes 98312 | tf_op jit(solution)/shard_map/ppermute | solution.py:274
  23.1 41.6 %collective-permute-start.4 = (f32[8,8,128]{2,1,0:T(8,128)S(1)}, f32[8,8,128]{2,1,0:T(8,128)S(1)}, u32[]{:S(2)}, u32[]{:S(2)}) collective-permute-start(f32[8,8,128]{2,1,0:T(8,128)S(1)} %shard_map.33), channel_id=1, source_target_pairs={{0,960},{128,256},{192,320},{256,192},{384,512},{448,576},{512,448... | collective-permute-start | bytes 98312 | tf_op jit(solution)/shard_map/ppermute | solution.py:274
  30.7 35.2 %collective-permute-start.5 = (f32[13,8,128]{2,1,0:T(8,128)S(1)}, f32[13,8,128]{2,1,0:T(8,128)S(1)}, u32[]{:S(2)}, u32[]{:S(2)}) collective-permute-start(f32[13,8,128]{2,1,0:T(8,128)S(1)} %get-tuple-element.12), channel_id=1, source_target_pairs={{0,64},{64,128},{128,192},{192,256},{256,320},{320,384},{384,448},... | collective-permute-start | bytes 159752 | tf_op jit(solution)/shard_map/ppermute | solution.py:274
  50.1 15.9 %collective-permute-start.6 = (f32[13,8,128]{2,1,0:T(8,128)S(1)}, f32[13,8,128]{2,1,0:T(8,128)S(1)}, u32[]{:S(2)}, u32[]{:S(2)}) collective-permute-start(f32[13,8,128]{2,1,0:T(8,128)S(1)} %get-tuple-element.13), channel_id=1, source_target_pairs={{0,960},{64,0},{128,64},{192,128},{256,192},{320,256},{384,320},{4... | collective-permute-start | bytes 159752 | tf_op jit(solution)/shard_map/ppermute | solution.py:274
  52.0 14.5 %collective-permute-start.9 = (f32[8,8,128]{2,1,0:T(8,128)S(1)}, f32[8,8,128]{2,1,0:T(8,128)S(1)}, u32[]{:S(2)}, u32[]{:S(2)}) collective-permute-start(f32[8,8,128]{2,1,0:T(8,128)S(1)} %collective-permute-done.7.refs_3_), channel_id=1, source_target_pairs={{128,192},{384,448},{640,704},{896,960},{129,193},{385,449},{641,7... | collective-permute-start | bytes 98312 | tf_op jit(solution)/shard_map/ppermute | solution.py:274
  64.7 14.5 %collective-permute-start.8 = (f32[8,8,128]{2,1,0:T(8,128)S(1)}, f32[8,8,128]{2,1,0:T(8,128)S(1)}, u32[]{:S(2)}, u32[]{:S(2)}) collective-permute-start(f32[8,8,128]{2,1,0:T(8,128)S(1)} %collective-permute-done.4.refs_0_), channel_id=1, source_target_pairs={{192,128},{448,384},{704,640},{960,896},{193,129},{449,385},{705,6... | collective-permute-start | bytes 98312 | tf_op jit(solution)/shard_map/ppermute | solution.py:274

commit v2 on v1

--- a/solution.py
+++ b/solution.py
@@ -202,10 +202,10 @@
     return tile
 
 
-def collide_kernel(pops_ref, zp_ref, zm_ref, first_ref, second_ref, came, out_ref):
+def collide(pops_ref, zp_ref, zm_ref, first_ref, second_ref, came, out_ref, places, start):
     columns = {1: (ZP, zp_ref[...]), -1: (ZM, zm_ref[...])}
     lines = y_lines(first_ref, second_ref)
-    for x in range(8):
+    for x in places:
         read = []
         for i, (cx, cy, cz) in enumerate(lattice_moves):
             source = x - cx
@@ -220,7 +220,7 @@
         common = 1.0 - 1.5 * (ux * ux + uy * uy + uz * uz)
         scaled = {w: (relaxation * w) * density for w in sorted(set(lattice_weights))}
         keep = 1.0 - relaxation
-        out_ref[0, x] = keep * read[0] + scaled[lattice_weights[0]] * common
+        out_ref[0, x - start] = keep * read[0] + scaled[lattice_weights[0]] * common
         for i in range(1, 19, 2):
             projected = None
             for c, u in zip(lattice_moves[i], (ux, uy, uz)):
@@ -230,8 +230,8 @@
             weight = scaled[lattice_weights[i]]
             even = weight * (common + 4.5 * projected * projected)
             odd = weight * (3.0 * projected)
-            out_ref[i, x] = keep * read[i] + (even + odd)
-            out_ref[i + 1, x] = keep * read[i + 1] + (even - odd)
+            out_ref[i, x - start] = keep * read[i] + (even + odd)
+            out_ref[i + 1, x - start] = keep * read[i + 1] + (even - odd)
 
 
 def post_kernel(load_ref, came, out_ref, parcels):
@@ -246,9 +246,14 @@
             out_ref[2 * half + k // 8, k % 8] = tile
 
 
-def last_kernel(pops_ref, zp_ref, zm_ref, first_ref, second_ref, load_ref, *refs):
+def inner_kernel(pops_ref, zp_ref, zm_ref, first_ref, second_ref, out_ref):
+    collide(pops_ref, zp_ref, zm_ref, first_ref, second_ref, (), out_ref, range(1, 7), 1)
+
+
+def last_kernel(pops_ref, zp_ref, zm_ref, first_ref, second_ref, load_ref, inner_ref, *refs):
     *came, next_ref, slab_ref, parcels = refs
-    collide_kernel(pops_ref, zp_ref, zm_ref, first_ref, second_ref, came, next_ref)
+    next_ref[:, 1:7] = inner_ref[...]
+    collide(pops_ref, zp_ref, zm_ref, first_ref, second_ref, came, next_ref, (0, 7), 0)
     post_kernel(load_ref, came, slab_ref, parcels)
 
 
@@ -300,10 +305,11 @@
     for kind, ways, first_step in LONG:
         sent = message[kind] if first_step is None else came[first_step]
         came.append(hop(sent, ways))
+    (inner,) = call(inner_kernel, [(19, 6, 8, 128)], (populations, zp, zm, first, second))
     return call(
         last_kernel,
         [(19, 8, 8, 128), (4, 8, 8, 128)],
-        (populations, zp, zm, first, second, load, *came),
+        (populations, zp, zm, first, second, load, inner, *came),
         [pltpu.VMEM((4, 8, 8, 128), f32)],
     )
 

time: 81 us -> 80.8 us (level)
    pallas_call x6 -> x7, Pallas kernels: 3.14 us -> 3.21 us  [call(): pl.pallas_call(kernel, out_shape=[jax.ShapeDtypeStruct(s, f32) for s in o...]
where the time goes in v2:
time: 80.8 us; the launch traced here: 80.4 us
  starting transfers between devices  61.1 us (76%)
  waiting for transfers between devices  14.2 us (18%)
  Pallas kernels  3.21 us (4%)
  local copies, waits for them, and re-layouts  1.07 us (1%)
    ppermute x6, starting transfers between devices, hop(): return lax.ppermute(x, 'gx', pairs)  43.9 us
    ppermute x6, waiting for transfers between devices, hop(): return lax.ppermute(x, 'gx', pairs)  12.9 us
    ppermute x2, starting transfers between devices, swap(): return lax.ppermute(x, 'gy', pairs + [(j, i) for i, j in pairs])  9.72 us
    all_to_all x1, starting transfers between devices, steps(): lax.all_to_all(load.reshape(4, 8192), 'gx', 0, 0, tiled=True, axis_index_...  4.46 us
    pallas_call x7, Pallas kernels, call(): pl.pallas_call(kernel, out_shape=[jax.ShapeDtypeStruct(s, f32) for s in o...  3.21 us
    ppermute x2, starting transfers between devices, shifted(): return lax.ppermute(x, axis, [(i, (i + by) % count) for i in range(count)])  2.96 us
  transfers between devices with their start and end apart: 11, of which 3 were waited for; matrix products, arithmetic and copies ran while one was open for 0% of the time, Pallas kernels for 1%

profile of v2, /device:TPU:704, one launch (start us, length us, event | category | flops | bytes accessed | tf_op | source)
XLA Modules:
  0.0 80.4 jit_solution(17671543048623311664)
XLA Ops:
  0.6 1.1 %copy-done = f32[19,8,8,128]{3,2,1,0:T(8,128)S(1)} copy-done((f32[19,8,8,128]{3,2,1,0:T(8,128)S(1)}, f32[19,8,8,128]{3,2,1,0:T(8,128)}, u32[]{:S(2)}) %copy-start) | copy-done | bytes 622616
  1.7 1.2 %shard_map.32 = f32[4,8,8,128]{3,2,1,0:T(8,128)} custom-call(f32[19,8,8,128]{3,2,1,0:T(8,128)S(1)} %copy-done), custom_call_target="tpu_custom_call" | custom-call | tf_op jit(solution)/shard_map/pallas_call | solution.py:262
  2.9 4.5 %all-to-all-start = ((f32[4,1,8192]{2,1,0:T(1,128)}), f32[4,1,8192]{2,1,0:T(1,128)S(1)}, u32[]{:S(2)}, u32[]{:S(2)}) async-start(f32[4,1,8192]{2,1,0:T(1,128)} %bitcast), calls=%async_computation | async-start | bytes 262144 | tf_op jit(solution)/shard_map/all_to_all | solution.py:292
  7.4 0.1 shard_map.30
  7.6 0.0 collective-permute-start
  7.6 2.9 %collective-permute-start.1 = (f32[8,128]{1,0:T(8,128)S(1)}, f32[8,128]{1,0:T(8,128)S(1)}, u32[]{:S(2)}, u32[]{:S(2)}) collective-permute-start(f32[8,128]{1,0:T(8,128)S(1)} %get-tuple-element.9), channel_id=1, source_target_pairs={{0,7},{1,0},{2,1},{3,2},{4,3},{5,4},{6,5},{7,6},{8,15},{9,8},{10,9... | collective-permute-start | bytes 12296 | tf_op jit(solution)/shard_map/ppermute | solution.py:274
  10.5 1.3 %collective-permute-done.zp_ref = f32[8,128]{1,0:T(8,128)S(1)} collective-permute-done((f32[8,128]{1,0:T(8,128)S(1)}, f32[8,128]{1,0:T(8,128)S(1)}, u32[]{:S(2)}, u32[]{:S(2)}) %collective-permute-start) | collective-permute-done | bytes 4128 | tf_op jit(solution)/shard_map/ppermute | solution.py:274
  11.8 0.0 collective-permute-done.1.zm_ref
  11.9 0.2 shard_map.31
  12.0 2.9 %collective-permute-start.2 = (f32[5,8,128]{2,1,0:T(8,128)S(1)}, f32[5,8,128]{2,1,0:T(8,128)S(1)}, u32[]{:S(2)}, u32[]{:S(2)}) collective-permute-start(f32[5,8,128]{2,1,0:T(8,128)S(1)} %get-tuple-element.10), channel_id=1, source_target_pairs={{56,0},{8,16},{24,32},{40,48},{0,56},{16,8},{32,24},{48,40},{57,1}... | collective-permute-start | bytes 61448 | tf_op jit(solution)/shard_map/ppermute | solution.py:284
  15.0 6.8 %collective-permute-start.3 = (f32[5,8,128]{2,1,0:T(8,128)S(1)}, f32[5,8,128]{2,1,0:T(8,128)S(1)}, u32[]{:S(2)}, u32[]{:S(2)}) collective-permute-start(f32[5,8,128]{2,1,0:T(8,128)S(1)} %get-tuple-element.11), channel_id=1, source_target_pairs={{0,8},{16,24},{32,40},{48,56},{8,0},{24,16},{40,32},{56,48},{1,9},... | collective-permute-start | bytes 61448 | tf_op jit(solution)/shard_map/ppermute | solution.py:284
  21.8 0.0 all-to-all-done
  21.8 1.3 %collective-permute-start.7 = (f32[8,8,128]{2,1,0:T(8,128)S(1)}, f32[8,8,128]{2,1,0:T(8,128)S(1)}, u32[]{:S(2)}, u32[]{:S(2)}) collective-permute-start(f32[8,8,128]{2,1,0:T(8,128)S(1)} %shard_map.34), channel_id=1, source_target_pairs={{64,128},{320,384},{576,640},{832,896},{65,129},{321,385},{577,641... | collective-permute-start | bytes 98312 | tf_op jit(solution)/shard_map/ppermute | solution.py:279
  23.1 7.5 %collective-permute-start.4 = (f32[8,8,128]{2,1,0:T(8,128)S(1)}, f32[8,8,128]{2,1,0:T(8,128)S(1)}, u32[]{:S(2)}, u32[]{:S(2)}) collective-permute-start(f32[8,8,128]{2,1,0:T(8,128)S(1)} %shard_map.34), channel_id=1, source_target_pairs={{0,960},{128,256},{192,320},{256,192},{384,512},{448,576},{512,448... | collective-permute-start | bytes 98312 | tf_op jit(solution)/shard_map/ppermute | solution.py:279
  30.6 0.0 collective-permute-done.2.first_ref
  30.6 0.1 shard_map.35
  30.7 19.3 %collective-permute-start.5 = (f32[13,8,128]{2,1,0:T(8,128)S(1)}, f32[13,8,128]{2,1,0:T(8,128)S(1)}, u32[]{:S(2)}, u32[]{:S(2)}) collective-permute-start(f32[13,8,128]{2,1,0:T(8,128)S(1)} %get-tuple-element.12), channel_id=1, source_target_pairs={{0,64},{64,128},{128,192},{192,256},{256,320},{320,384},{384,448},... | collective-permute-start | bytes 159752 | tf_op jit(solution)/shard_map/ppermute | solution.py:279
  50.1 1.9 %collective-permute-start.6 = (f32[13,8,128]{2,1,0:T(8,128)S(1)}, f32[13,8,128]{2,1,0:T(8,128)S(1)}, u32[]{:S(2)}, u32[]{:S(2)}) collective-permute-start(f32[13,8,128]{2,1,0:T(8,128)S(1)} %get-tuple-element.13), channel_id=1, source_target_pairs={{0,960},{64,0},{128,64},{192,128},{256,192},{320,256},{384,320},{4... | collective-permute-start | bytes 159752 | tf_op jit(solution)/shard_map/ppermute | solution.py:279
  52.0 12.6 %collective-permute-start.9 = (f32[8,8,128]{2,1,0:T(8,128)S(1)}, f32[8,8,128]{2,1,0:T(8,128)S(1)}, u32[]{:S(2)}, u32[]{:S(2)}) collective-permute-start(f32[8,8,128]{2,1,0:T(8,128)S(1)} %collective-permute-done.7.refs_3_), channel_id=1, source_target_pairs={{128,192},{384,448},{640,704},{896,960},{129,193},{385,449},{641,7... | collective-permute-start | bytes 98312 | tf_op jit(solution)/shard_map/ppermute | solution.py:279
  64.7 1.3 %collective-permute-start.8 = (f32[8,8,128]{2,1,0:T(8,128)S(1)}, f32[8,8,128]{2,1,0:T(8,128)S(1)}, u32[]{:S(2)}, u32[]{:S(2)}) collective-permute-start(f32[8,8,128]{2,1,0:T(8,128)S(1)} %collective-permute-done.4.refs_0_), channel_id=1, source_target_pairs={{192,128},{448,384},{704,640},{960,896},{193,129},{449,385},{705,6... | collective-permute-start | bytes 98312 | tf_op jit(solution)/shard_map/ppermute | solution.py:279
  66.0 0.3 shard_map.33.inner_ref
  66.3 0.2 collective-permute-done.9.refs_5_
  66.5 12.7 %collective-permute-done.8.refs_4_ = f32[8,8,128]{2,1,0:T(8,128)S(1)} collective-permute-done((f32[8,8,128]{2,1,0:T(8,128)S(1)}, f32[8,8,128]{2,1,0:T(8,128)S(1)}, u32[]{:S(2)}, u32[]{:S(2)}) %collective-permute-start.8) | collective-permute-done | bytes 32800 | tf_op jit(solution)/shard_map/ppermute | solution.py:279
  79.2 1.2 %shard_map.36 = (f32[19,8,8,128]{3,2,1,0:T(8,128)}, f32[4,8,8,128]{3,2,1,0:T(8,128)}) custom-call(f32[19,8,8,128]{3,2,1,0:T(8,128)S(1)} %copy-done.1, f32[8,128]{1,0:T(8,128)S(1)} %collective-permute-done.zp_ref, f32[8,128]{1,0:T(8,128)S(1)} %collective-permute-done.1.zm_ref, f32[5,8,128]{2,1,0:T(8,128)S(1)} %collective-permute-done.2.first_ref, ...), custom_call_target="tpu_custom_call" | custom-call | tf_op jit(solution)/shard_map/pallas_call | solution.py:262
  (9 shorter events, 0.0 us)
Async XLA Ops:
  0.6 1.1 %copy-start = (f32[19,8,8,128]{3,2,1,0:T(8,128)S(1)}, f32[19,8,8,128]{3,2,1,0:T(8,128)}, u32[]{:S(2)}) copy-start(f32[19,8,8,128]{3,2,1,0:T(8,128)} %pops_ref.11) | copy-start | bytes 1867780
  1.7 5.7 %copy-start.1 = (f32[19,8,8,128]{3,2,1,0:T(8,128)S(1)}, f32[19,8,8,128]{3,2,1,0:T(8,128)}, u32[]{:S(2)}) copy-start(f32[19,8,8,128]{3,2,1,0:T(8,128)} %pops_ref.11) | copy-start | bytes 1867780
  2.9 18.8 %all-to-all-start = ((f32[4,1,8192]{2,1,0:T(1,128)}), f32[4,1,8192]{2,1,0:T(1,128)S(1)}, u32[]{:S(2)}, u32[]{:S(2)}) async-start(f32[4,1,8192]{2,1,0:T(1,128)} %bitcast), calls=%async_computation | async-start | bytes 262144 | tf_op jit(solution)/shard_map/all_to_all | solution.py:292
  7.6 4.3 %collective-permute-start = (f32[8,128]{1,0:T(8,128)S(1)}, f32[8,128]{1,0:T(8,128)S(1)}, u32[]{:S(2)}, u32[]{:S(2)}) collective-permute-start(f32[8,128]{1,0:T(8,128)S(1)} %get-tuple-element.8), channel_id=1, source_target_pairs={{0,1},{1,2},{2,3},{3,4},{4,5},{5,6},{6,7},{7,0},{8,9},{9,10},{10,1... | collective-permute-start | bytes 12296 | tf_op jit(solution)/shard_map/ppermute | solution.py:274
  7.6 4.3 %collective-permute-start.1 = (f32[8,128]{1,0:T(8,128)S(1)}, f32[8,128]{1,0:T(8,128)S(1)}, u32[]{:S(2)}, u32[]{:S(2)}) collective-permute-start(f32[8,128]{1,0:T(8,128)S(1)} %get-tuple-element.9), channel_id=1, source_target_pairs={{0,7},{1,0},{2,1},{3,2},{4,3},{5,4},{6,5},{7,6},{8,15},{9,8},{10,9... | collective-permute-start | bytes 12296 | tf_op jit(solution)/shard_map/ppermute | solution.py:274
  12.0 18.5 %collective-permute-start.2 = (f32[5,8,128]{2,1,0:T(8,128)S(1)}, f32[5,8,128]{2,1,0:T(8,128)S(1)}, u32[]{:S(2)}, u32[]{:S(2)}) collective-permute-start(f32[5,8,128]{2,1,0:T(8,128)S(1)} %get-tuple-element.10), channel_id=1, source_target_pairs={{56,0},{8,16},{24,32},{40,48},{0,56},{16,8},{32,24},{48,40},{57,1}... | collective-permute-start | bytes 61448 | tf_op jit(solution)/shard_map/ppermute | solution.py:284
  15.0 15.6 %collective-permute-start.3 = (f32[5,8,128]{2,1,0:T(8,128)S(1)}, f32[5,8,128]{2,1,0:T(8,128)S(1)}, u32[]{:S(2)}, u32[]{:S(2)}) collective-permute-start(f32[5,8,128]{2,1,0:T(8,128)S(1)} %get-tuple-element.11), channel_id=1, source_target_pairs={{0,8},{16,24},{32,40},{48,56},{8,0},{24,16},{40,32},{56,48},{1,9},... | collective-permute-start | bytes 61448 | tf_op jit(solution)/shard_map/ppermute | solution.py:284
  21.8 30.2 %collective-permute-start.7 = (f32[8,8,128]{2,1,0:T(8,128)S(1)}, f32[8,8,128]{2,1,0:T(8,128)S(1)}, u32[]{:S(2)}, u32[]{:S(2)}) collective-permute-start(f32[8,8,128]{2,1,0:T(8,128)S(1)} %shard_map.34), channel_id=1, source_target_pairs={{64,128},{320,384},{576,640},{832,896},{65,129},{321,385},{577,641... | collective-permute-start | bytes 98312 | tf_op jit(solution)/shard_map/ppermute | solution.py:279
  23.1 41.6 %collective-permute-start.4 = (f32[8,8,128]{2,1,0:T(8,128)S(1)}, f32[8,8,128]{2,1,0:T(8,128)S(1)}, u32[]{:S(2)}, u32[]{:S(2)}) collective-permute-start(f32[8,8,128]{2,1,0:T(8,128)S(1)} %shard_map.34), channel_id=1, source_target_pairs={{0,960},{128,256},{192,320},{256,192},{384,512},{448,576},{512,448... | collective-permute-start | bytes 98312 | tf_op jit(solution)/shard_map/ppermute | solution.py:279
  30.7 35.5 %collective-permute-start.5 = (f32[13,8,128]{2,1,0:T(8,128)S(1)}, f32[13,8,128]{2,1,0:T(8,128)S(1)}, u32[]{:S(2)}, u32[]{:S(2)}) collective-permute-start(f32[13,8,128]{2,1,0:T(8,128)S(1)} %get-tuple-element.12), channel_id=1, source_target_pairs={{0,64},{64,128},{128,192},{192,256},{256,320},{320,384},{384,448},... | collective-permute-start | bytes 159752 | tf_op jit(solution)/shard_map/ppermute | solution.py:279
  50.1 16.2 %collective-permute-start.6 = (f32[13,8,128]{2,1,0:T(8,128)S(1)}, f32[13,8,128]{2,1,0:T(8,128)S(1)}, u32[]{:S(2)}, u32[]{:S(2)}) collective-permute-start(f32[13,8,128]{2,1,0:T(8,128)S(1)} %get-tuple-element.13), channel_id=1, source_target_pairs={{0,960},{64,0},{128,64},{192,128},{256,192},{320,256},{384,320},{4... | collective-permute-start | bytes 159752 | tf_op jit(solution)/shard_map/ppermute | solution.py:279
  52.0 14.5 %collective-permute-start.9 = (f32[8,8,128]{2,1,0:T(8,128)S(1)}, f32[8,8,128]{2,1,0:T(8,128)S(1)}, u32[]{:S(2)}, u32[]{:S(2)}) collective-permute-start(f32[8,8,128]{2,1,0:T(8,128)S(1)} %collective-permute-done.7.refs_3_), channel_id=1, source_target_pairs={{128,192},{384,448},{640,704},{896,960},{129,193},{385,449},{641,7... | collective-permute-start | bytes 98312 | tf_op jit(solution)/shard_map/ppermute | solution.py:279
  64.7 14.5 %collective-permute-start.8 = (f32[8,8,128]{2,1,0:T(8,128)S(1)}, f32[8,8,128]{2,1,0:T(8,128)S(1)}, u32[]{:S(2)}, u32[]{:S(2)}) collective-permute-start(f32[8,8,128]{2,1,0:T(8,128)S(1)} %collective-permute-done.4.refs_0_), channel_id=1, source_target_pairs={{192,128},{448,384},{704,640},{960,896},{193,129},{449,385},{705,6... | collective-permute-start | bytes 98312 | tf_op jit(solution)/shard_map/ppermute | solution.py:279
